TPU v7x, 256 devices: a whole 4x4x8 slice. The times are simulated.
256 devices in a mesh: row: 32 (over x, z), col: 8 (over y, core).
Axes of the slice: x: 4, y: 4, z: 8, core: 2. Of those that a mesh axis runs over, the one named last changes fastest.
Arguments:
- diag_tiles: float32 [32, 512, 512], P('row', 'col'), as said below
- sub_tiles: float32 [32, 512, 512], P('row', 'col')
- boundary: float32 [512, 512], P('col'), as said below
Outputs:
- inverse_blocks: float32 [32, 512, 512], P('row', 'col')
Inputs may be any that keep to these rules, and one draw needn't show every extreme that they name: `diag_tiles`: every tile is lower triangular, zero above the diagonal, with diagonal entries between 0.2 and 0.4. `boundary`: symmetric positive definite, smallest eigenvalue at least 2.
All inputs are finite; a program needn't handle non-finite values.
Results may differ from a plain program's by a relative error of at most 0.0003.
Values sent between devices are 32-bit elements; how exact they have to be, the bound alone decides.
A program may use at most 256 MiB of HBM per device.

v0:
```python
import jax
import jax.numpy as jnp
from jax import lax
from jax.sharding import Mesh
from jax.sharding import PartitionSpec as P

ROW = ("row_0", "row_1")


def gather_turned(arrays, axis, dims):
    turned = [jnp.moveaxis(a, dim, 0) for a, dim in zip(arrays, dims)]
    widths = [t[0].size for t in turned]
    both = jnp.concatenate([t.reshape(-1, w) for t, w in zip(turned, widths)], axis=1)
    out = lax.all_gather(both, axis, axis=0, tiled=True)
    pieces = jnp.split(out, [sum(widths[:k]) for k in range(1, len(widths))], axis=1)
    return tuple(
        (
            jnp.moveaxis(b.reshape(-1, *t.shape[1:]), 0, dim)
            for b, t, dim in zip(pieces, turned, dims)
        )
    )


def nothing_yet(array, identity):
    return jax.tree.map(
        lambda part, zero: jnp.zeros_like(part) + jnp.asarray(zero, part.dtype), array, identity
    )


def prefix_by_axis(array, axes, combine, identity):
    before = start = nothing_yet(array, identity)
    so_far = array
    for axis in reversed(axes):
        length, place = (lax.axis_size(axis), lax.axis_index(axis))
        pieces = jax.tree.map(lambda part: lax.all_gather(part, axis), so_far)
        inside, so_far = (start, start)
        for k in reversed(range(length)):
            passed = k > place
            so_far = combine(so_far, jax.tree.map(lambda part: part[k], pieces))
            inside = jax.tree.map(lambda new, old: jnp.where(passed, new, old), so_far, inside)
        before = combine(inside, before)
    return before


def product(left, right):
    return jnp.dot(left, right, precision=lax.Precision.HIGHEST)


def advance(weight_block, inner_block, local_block):
    return local_block + product(weight_block.T, product(inner_block, weight_block))


def compose(earlier, later):
    earlier_sum, earlier_map = earlier
    later_sum, later_map = later
    return (
        later_sum + product(later_map.T, product(earlier_sum, later_map)),
        product(earlier_map, later_map),
    )


def on_device(diag_tiles, sub_tiles, boundary):
    slice_rows = diag_tiles.shape[1]
    first_row = lax.axis_index("col") * slice_rows
    inverse_all, coupling_all, end_block = gather_turned(
        (diag_tiles, sub_tiles, boundary), "col", (1, 1, 0)
    )
    blocks_here = inverse_all.shape[0]
    tile_size = inverse_all.shape[2]
    identity_map = jnp.eye(tile_size, dtype=jnp.float32)
    local_terms = jnp.einsum(
        "bki,bkj->bij", inverse_all, inverse_all, precision=lax.Precision.HIGHEST
    )
    weights = jnp.einsum("bik,bkj->bij", coupling_all, inverse_all, precision=lax.Precision.HIGHEST)
    folded_sum = local_terms[blocks_here - 1]
    folded_map = weights[blocks_here - 1]
    zero_sum = jnp.zeros((tile_size, tile_size), jnp.float32)
    entry_sum, entry_map = prefix_by_axis(
        (folded_sum, folded_map), ROW, compose, (zero_sum, identity_map)
    )
    current = entry_sum + product(entry_map.T, product(end_block, entry_map))
    results = [current] * blocks_here
    current = advance(weights[0], current, local_terms[0])
    results[0] = lax.dynamic_slice_in_dim(current, first_row, slice_rows, 0)
    return jnp.stack(results)


def solution(mesh):
    finer = Mesh(mesh.devices.reshape(4, 8, mesh.shape["col"]), ("row_0", "row_1", "col"))
    return jax.shard_map(
        on_device,
        mesh=finer,
        in_specs=(P(ROW, "col", None), P(ROW, "col", None), P("col", None)),
        out_specs=P(ROW, "col", None),
        check_vma=False,
    )
```

profile of v0, /device:TPU:1, one launch (start us, length us, event | category | flops | bytes accessed | tf_op | source)
XLA Modules:
  0.0 388.0 jit_solution(3145122074323205898)
XLA Ops:
  8.4 35.2 %all-gather.10.cloned.1.call-done = f32[512,1536]{1,0:T(8,128)} async-done(((f32[64,1536]{1,0:T(8,128)}), f32[512,1536]{1,0:T(8,128)}) %all-gather.10.cloned.1.call-update) | async-done | bytes 3145744 | tf_op jit(solution)/shard_map/all_gather | solution.py:14
  43.6 4.5 %fusion.14 = f32[512,512]{1,0:T(8,128)} fusion(f32[512,1536]{1,0:T(8,128)} %all-gather.10.cloned.1.call-done), kind=kOutput, calls=%fused_computation.30 | convolution fusion | flops 1610612736 | bytes 3145728 | tf_op jit(solution)/shard_map/bik,bkj->bij/dot_general | solution.py:74
  48.2 4.4 %fusion.29 = f32[512,512]{1,0:T(8,128)} fusion(f32[512,1536]{1,0:T(8,128)} %all-gather.10.cloned.1.call-done), kind=kOutput, calls=%fused_computation.48 | convolution fusion | flops 1610612736 | bytes 2097152 | tf_op jit(solution)/shard_map/bki,bkj->bij/dot_general | solution.py:71
  53.0 88.7 %all-gather.14.cloned.1.call-done = f32[4096,512]{1,0:T(8,128)} async-done(((f32[512,512]{1,0:T(8,128)}), f32[4096,512]{1,0:T(8,128)}) %all-gather.14.cloned.1.call-update) | async-done | bytes 8388624 | tf_op jit(solution)/shard_map/all_gather | solution.py:35
  141.7 2.4 fusion.26
  144.2 3.7 fusion.52
  147.9 3.1 fusion.57
  151.0 3.1 fusion.62
  163.6 3.4 fusion.82
  168.5 67.8 %all-gather.12.cloned.1.call-done = f32[4096,512]{1,0:T(8,128)} async-done(((f32[512,512]{1,0:T(8,128)}), f32[4096,512]{1,0:T(8,128)}) %all-gather.12.cloned.1.call-update) | async-done | bytes 8388624 | tf_op jit(solution)/shard_map/all_gather | solution.py:35
  236.3 3.5 convolution_add_fusion.13
  239.8 3.7 fusion.50
  243.5 3.5 convolution_add_fusion.12
  247.1 3.5 fusion.55
  250.6 3.2 convolution_add_fusion.11
  255.7 2.0 convolution_add_fusion.10
  267.1 2.1 convolution_add_fusion.7
  271.1 2.9 convolution_add_fusion.6
  274.0 4.1 %fusion.16 = f32[512,512]{1,0:T(8,128)S(1)} fusion(f32[512,512]{1,0:T(8,128)} %convolution_add_fusion.6, f32[512,512]{1,0:T(8,128)} %copy-done.13, f32[512,512]{1,0:T(8,128)} %copy-done.12, f32[512,512]{1,0:T(8,128)} %copy-done.11, f32[512,512]{1,0:T(8,128)} %copy-done.10, f32[512,512]{1,0:T(8,128)} %copy-done.9, f32[512,512]{1,0:T(8,128)} %copy-done.8, ...), kind=kOutput, calls=%fused_computation.33 | convolution fusion | flops 1612972032 | bytes 9437192 | tf_op jit(solution)/shard_map/dot_general | solution.py:46
  278.1 2.1 fusion.27
  280.1 3.8 fusion.8
  283.9 3.4 all-gather.18.cloned.1.call-done
  288.6 51.5 %all-gather.16.cloned.1.call-done = f32[2048,512]{1,0:T(8,128)} async-done(((f32[512,512]{1,0:T(8,128)}), f32[2048,512]{1,0:T(8,128)}) %all-gather.16.cloned.1.call-update) | async-done | bytes 4194320 | tf_op jit(solution)/shard_map/all_gather | solution.py:35
  340.1 3.6 convolution_add_fusion.5
  343.6 3.1 fusion.34
  346.7 3.9 convolution_add_fusion.4
  352.4 1.9 convolution_add_fusion.3
  356.2 2.0 fusion
  361.1 2.0 fusion.36
  365.0 1.9 convolution_select_fusion
  370.7 3.1 fusion.12
  375.7 2.1 fusion.107
  (72 shorter events, 45.0 us)
Async XLA Ops:
  6.5 37.1 %all-gather.10.cloned.1.call-start = ((), (), s32[]{:S(2)}) async-start(), calls=%async_computation | async-start | bytes 3538944 | tf_op jit(solution)/shard_map/all_gather | solution.py:14
  8.4 133.4 %all-gather.14.cloned.1.call-start = ((), (), s32[]{:S(2)}) async-start(), calls=%async_computation.2 | async-start | bytes 9437184 | tf_op jit(solution)/shard_map/all_gather | solution.py:35
  48.1 188.1 %all-gather.12.cloned.1.call-start = ((), (), s32[]{:S(2)}) async-start(), calls=%async_computation.1 | async-start | bytes 9437184 | tf_op jit(solution)/shard_map/all_gather | solution.py:35
  52.7 234.6 %all-gather.18.cloned.1.call-start = ((), (), s32[]{:S(2)}) async-start(), calls=%async_computation.4 | async-start | bytes 5242880 | tf_op jit(solution)/shard_map/all_gather | solution.py:35
  141.7 13.3 %copy-start = (f32[4096,512]{1,0:T(8,128)S(1)}, f32[4096,512]{1,0:T(8,128)}, u32[]{:S(2)}) copy-start(f32[4096,512]{1,0:T(8,128)} %all-gather.14.cloned.1.call-done) | copy-start | bytes 25165828
  144.2 3.7 copy-start.7
  154.0 1.0 copy-start.3
  156.9 1.0 copy-start.4
  159.8 1.0 copy-start.5
  162.6 1.0 copy-start.6
  167.1 173.0 %all-gather.16.cloned.1.call-start = ((), (), s32[]{:S(2)}) async-start(), calls=%async_computation.3 | async-start | bytes 5242880 | tf_op jit(solution)/shard_map/all_gather | solution.py:35
  236.3 14.4 %copy-start.14 = (f32[4096,512]{1,0:T(8,128)S(1)}, f32[4096,512]{1,0:T(8,128)}, u32[]{:S(2)}) copy-start(f32[4096,512]{1,0:T(8,128)} %all-gather.12.cloned.1.call-done) | copy-start | bytes 25165828
  236.3 17.6 %slice-start = ((s8[8388608]{0:T(1024)(128)(4,1)}), s8[4194304]{0:T(1024)(128)(4,1)S(1)}, s32[]{:S(2)}) async-start(s8[8388608]{0:T(1024)(128)(4,1)} %bitcast.48), calls=%async_computation.5 | async-start | bytes 8388608
  243.5 10.3 %slice-start.1 = ((s8[8388608]{0:T(1024)(128)(4,1)}), s8[4194304]{0:T(1024)(128)(4,1)S(1)}, s32[]{:S(2)}) async-start(s8[8388608]{0:T(1024)(128)(4,1)} %bitcast.48), calls=%async_computation.6 | async-start | bytes 8388608
  247.1 12.5 %copy-start.8 = (f32[512,512]{1,0:T(8,128)}, f32[512,512]{1,0:T(8,128)S(1)}, u32[]{:S(2)}) copy-start(f32[512,512]{1,0:T(8,128)S(1)} %convolution_add_fusion.12) | copy-start | bytes 3145732
  253.9 9.5 %copy-start.9 = (f32[512,512]{1,0:T(8,128)}, f32[512,512]{1,0:T(8,128)S(1)}, u32[]{:S(2)}) copy-start(f32[512,512]{1,0:T(8,128)S(1)} %convolution_add_fusion.11) | copy-start | bytes 3145732
  257.8 9.3 %copy-start.10 = (f32[512,512]{1,0:T(8,128)}, f32[512,512]{1,0:T(8,128)S(1)}, u32[]{:S(2)}) copy-start(f32[512,512]{1,0:T(8,128)S(1)} %convolution_add_fusion.10) | copy-start | bytes 3145732
  261.5 9.6 %copy-start.11 = (f32[512,512]{1,0:T(8,128)}, f32[512,512]{1,0:T(8,128)S(1)}, u32[]{:S(2)}) copy-start(f32[512,512]{1,0:T(8,128)S(1)} %convolution_add_fusion.9) | copy-start | bytes 3145732
  265.2 3.9 %copy-start.12 = (f32[512,512]{1,0:T(8,128)}, f32[512,512]{1,0:T(8,128)S(1)}, u32[]{:S(2)}) copy-start(f32[512,512]{1,0:T(8,128)S(1)} %convolution_add_fusion.8) | copy-start | bytes 3145732
  269.2 1.9 copy-start.13
  340.1 10.5 %copy-start.1 = (f32[2048,512]{1,0:T(8,128)S(1)}, f32[2048,512]{1,0:T(8,128)}, u32[]{:S(2)}) copy-start(f32[2048,512]{1,0:T(8,128)} %all-gather.18.cloned.1.call-done) | copy-start | bytes 12582916
  340.1 12.4 %copy-start.16 = (f32[2048,512]{1,0:T(8,128)S(1)}, f32[2048,512]{1,0:T(8,128)}, u32[]{:S(2)}) copy-start(f32[2048,512]{1,0:T(8,128)} %all-gather.16.cloned.1.call-done) | copy-start | bytes 12582916
  360.1 8.8 %copy-start.15 = (f32[512,512]{1,0:T(8,128)S(1)}, f32[512,512]{1,0:T(8,128)}, u32[]{:S(2)}) copy-start(f32[512,512]{1,0:T(8,128)} %fusion.27) | copy-start | bytes 3145732
  367.0 8.7 %copy-start.2 = (f32[512,512]{1,0:T(8,128)S(1)}, f32[512,512]{1,0:T(8,128)}, u32[]{:S(2)}) copy-start(f32[512,512]{1,0:T(8,128)} %fusion.14) | copy-start | bytes 3145732
Sparse Core Ops, SparseCore 0:
  9.2 34.4 all-gather.9
  48.3 93.4 all-gather.13
  143.5 92.6 all-gather.11
  237.9 49.3 all-gather.17
  288.9 51.0 all-gather.15
where the time goes:
time: 392 us; the launch traced here: 388 us
  waiting for transfers between devices  247 us (63%)
  matrix products  117 us (30%)
  between operations  13.9 us (4%)
  other arithmetic  6.09 us (2%)
  local copies, waits for them, and re-layouts  4.02 us (1%)
    all_gather x4, waiting for transfers between devices, prefix_by_axis(): pieces = jax.tree.map(lambda part: lax.all_gather(part, axis), so_far)  211 us
    dot_general x44, matrix products, product(): return jnp.dot(left, right, precision=lax.Precision.HIGHEST)  108 us
    all_gather x1, waiting for transfers between devices, gather_turned(): out = lax.all_gather(both, axis, axis=0, tiled=True)  35.2 us
  transfers between devices with their start and end apart: 5, of which 5 were waited for; matrix products, arithmetic and copies ran while one was open for 20% of the time, Pallas kernels for 0%

commit v1 on v0

v1 whole, which is shorter than its diff:
```python
import functools

import jax
import jax.numpy as jnp
from jax import lax
from jax.experimental import pallas as pl
from jax.experimental.pallas import tpu as pltpu

MESH = pl.DeviceIdType.MESH
BF16 = jnp.bfloat16
F32 = jnp.float32


def split(value):
    high = value.astype(BF16)
    low = (value - high.astype(F32)).astype(BF16)
    return high, low


def dot(left, right):
    return jnp.dot(left, right, preferred_element_type=F32)


def product3(left_high, left_low, right_high, right_low):
    rows = left_high.shape[0]
    both = dot(jnp.concatenate([left_high, left_low], axis=0), right_high)
    return both[:rows] + both[rows:] + dot(left_high, right_low)


def kernel(
    rows_total, levels, d_ref, s_ref, b_ref, o_ref,
    full, entry, sums, ends, landed, m_high, m_low, t_high, t_low,
    full_sem, entry_sem, misc_sem, send_sem,
):
    size = d_ref.shape[-1]
    piece = size // 8
    block = size // 4
    row = lax.axis_index("row")
    col = lax.axis_index("col")
    ring = col // 2
    core = col % 2
    right = (ring + 1) % 4
    left = (ring + 3) % 4
    across = (ring + 2) % 4
    partner = (row, 2 * ring + (1 - core))

    def at_ring(place):
        return (row, 2 * place + core)

    def piece_rows(number):
        return pl.ds(pl.multiple_of(number * piece, piece), piece)

    def part(array, number):
        return full.at[array, piece_rows(number)]

    def copy(src, dst, send, recv, device):
        return pltpu.make_async_remote_copy(
            src_ref=src, dst_ref=dst, send_sem=send, recv_sem=recv,
            device_id=device, device_id_type=MESH,
        )

    some = full.at[0, pl.ds(0, piece)]

    def wait_sent(stage, *numbers):
        for number in numbers:
            copy(some, some, send_sem.at[stage, number], misc_sem.at[0], partner).wait_send()

    def wait_part(array, number):
        here = part(array, number)
        copy(here, here, send_sem.at[0, 0], full_sem.at[array, number], partner).wait_recv()

    def wait_entry(stage, half):
        here = entry.at[stage, pl.ds(half * piece, piece)]
        copy(here, here, send_sem.at[0, 0], entry_sem.at[stage, half], partner).wait_recv()

    def send_part(array, number, device, stage, sem):
        here = part(array, number)
        copy(here, here, send_sem.at[stage, sem], full_sem.at[array, number], device).start()

    barrier = pltpu.get_barrier_semaphore()
    greeted = [partner, at_ring(right), at_ring(left)]
    for level in range(levels):
        step = 2**level
        greeted.append(((row + step) % rows_total, col))
        greeted.append(((row + rows_total - step) % rows_total, col))
    for device in greeted:
        pl.semaphore_signal(barrier, inc=1, device_id=device, device_id_type=MESH)
    pl.semaphore_wait(barrier, len(greeted))

    begin = levels + 2
    mine = 2 * ring + core
    forth = (ring + 1 + 2 * core) % 4
    back = (ring + 3 + 2 * core) % 4
    for sem, device in enumerate((at_ring(forth), at_ring(back), partner)):
        copy(d_ref.at[0], part(0, mine), send_sem.at[begin, sem], full_sem.at[0, mine], device).start()

    @pl.when(core == 1)
    def _():
        copy(
            s_ref.at[0], entry.at[0, pl.ds(piece, piece)],
            send_sem.at[begin, 7], entry_sem.at[0, 1], partner,
        ).start()

    own_ends = ends.at[piece_rows(core)]
    copy(b_ref, own_ends, send_sem.at[begin, 8], misc_sem.at[1], partner).start()
    full[0, piece_rows(mine)] = d_ref[0]
    ends[piece_rows(core)] = b_ref[...]
    wait_part(0, 2 * back + core)
    send_part(0, 2 * back + core, at_ring(forth), begin, 3)
    send_part(0, 2 * back + core, partner, begin, 4)
    wait_part(0, 2 * forth + core)
    send_part(0, 2 * forth + core, partner, begin, 5)
    wait_part(0, 2 * across + core)
    send_part(0, 2 * across + core, partner, begin, 6)
    for place in (ring, back, forth, across):
        wait_part(0, 2 * place + (1 - core))
    other_ends = ends.at[piece_rows(1 - core)]
    copy(other_ends, other_ends, send_sem.at[0, 0], misc_sem.at[1], partner).wait_recv()

    def split_full(array):
        for number in range(4):
            rows = pl.ds(number * block, block)
            m_high[rows], m_low[rows] = split(full[array, rows])

    def split_turned(array):
        columns = pl.ds(pl.multiple_of(ring * block, block), block)
        t_high[...], t_low[...] = split(full[array, :, columns].T)

    def times_full(value):
        high, low = split(value)
        return product3(high, low, m_high[...], m_low[...])

    def spread(array, half, stage):
        number = 2 * ring + half
        send_part(array, number, at_ring(right), stage, 2 * half)
        send_part(array, number, at_ring(left), stage, 2 * half + 1)

    @pl.when(core == 0)
    def _():
        def stage_of_maps(stage, source):
            array = stage + 1
            split_full(min(stage, levels + 1))
            step = 2**stage
            for half in range(2):
                value = times_full(source(half))
                number = 2 * ring + half
                full[array, piece_rows(number)] = value
                spread(array, half, stage)
                if stage < levels:
                    @pl.when(row >= step)
                    def _():
                        copy(
                            part(array, number), entry.at[stage + 1, pl.ds(half * piece, piece)],
                            send_sem.at[stage, 14 + half], entry_sem.at[stage + 1, half],
                            (row - step, col),
                        ).start()
                send_part(array, number, partner, stage, 6 + half)
            wait_part(array, 2 * left)
            send_part(array, 2 * left, at_ring(right), stage, 4)
            send_part(array, 2 * left, partner, stage, 8)
            wait_part(array, 2 * right + 1)
            send_part(array, 2 * right + 1, at_ring(left), stage, 5)
            send_part(array, 2 * right + 1, partner, stage, 9)
            for sem, number in enumerate(
                (2 * left + 1, 2 * right, 2 * across, 2 * across + 1), start=10
            ):
                wait_part(array, number)
                send_part(array, number, partner, stage, sem)

        def sent(stage):
            wait_sent(stage, *range(14))
            if stage < levels:
                @pl.when(row >= 2**stage)
                def _():
                    wait_sent(stage, 14, 15)

        def first(half):
            if half == 0:
                return s_ref[0]
            wait_entry(0, 1)
            return entry[0, pl.ds(piece, piece)]

        stage_of_maps(0, first)
        for stage in range(1, levels + 1):
            @pl.when(row + 2**stage <= rows_total)
            def _(stage=stage):
                def arrived(half):
                    wait_entry(stage, half)
                    return entry[stage, pl.ds(half * piece, piece)]

                stage_of_maps(stage, arrived)

        @pl.when(row == 0)
        def _():
            stage_of_maps(levels + 1, lambda half: ends[pl.ds(half * piece, piece)])

        sent(0)
        for stage in range(1, levels + 1):
            @pl.when(row + 2**stage <= rows_total)
            def _(stage=stage):
                sent(stage)

        @pl.when(row == 0)
        def _():
            sent(levels + 1)

        wait_sent(begin, *range(7), 8)
        copy(landed, landed, send_sem.at[0, 0], misc_sem.at[2], partner).wait_recv()
        o_ref[0] = landed[...]

    @pl.when(core == 1)
    def _():
        first_array = levels + 2

        def pass_on(stage, half):
            step = 2**stage

            @pl.when(row >= step)
            def _():
                copy(
                    sums.at[stage, pl.ds(half * piece, piece)],
                    entry.at[stage + 1, pl.ds(half * piece, piece)],
                    send_sem.at[stage, 14 + half], entry_sem.at[stage + 1, half],
                    (row - step, col),
                ).start()

        split_full(0)
        split_turned(0)
        sums[0] = product3(t_high[...], t_low[...], m_high[...], m_low[...])
        pass_on(0, 0)
        pass_on(0, 1)

        for stage in range(1, levels + 1):
            step = 2 ** (stage - 1)
            array = first_array + stage

            @pl.when(row + step <= rows_total)
            def _(stage=stage, step=step, array=array):
                for number in range(8):
                    wait_part(stage, number)
                split_full(stage)
                split_turned(stage)

                @pl.when(row + step == rows_total)
                def _():
                    entry[stage] = ends[...]

                for half in range(2):
                    @pl.when(row + step < rows_total)
                    def _():
                        wait_entry(stage, half)

                    full[array, piece_rows(2 * ring + half)] = times_full(
                        entry[stage, pl.ds(half * piece, piece)]
                    )
                    spread(array, half, stage)

                def term(place):
                    rows = pl.ds(pl.multiple_of(place * block, block), block)
                    high, low = split(full[array, rows])
                    return product3(t_high[:, rows], t_low[:, rows], high, low)

                total = sums[stage - 1] + term(ring)
                wait_part(array, 2 * left)
                send_part(array, 2 * left, at_ring(right), stage, 4)
                wait_part(array, 2 * right + 1)
                send_part(array, 2 * right + 1, at_ring(left), stage, 5)
                wait_part(array, 2 * left + 1)
                total = total + term(left)
                wait_part(array, 2 * right)
                total = total + term(right)
                wait_part(array, 2 * across)
                wait_part(array, 2 * across + 1)
                sums[stage] = total + term(across)

            @pl.when(row + step > rows_total)
            def _(stage=stage):
                sums[stage] = sums[stage - 1]

            if stage < levels:
                pass_on(stage, 0)
                pass_on(stage, 1)

        @pl.when(row == 0)
        def _():
            for number in range(8):
                wait_part(levels + 1, number)
            split_turned(levels + 1)
            for number in range(8):
                wait_part(levels + 2, number)
            split_full(levels + 2)
            sums[levels] = sums[levels] + product3(
                t_high[...], t_low[...], m_high[...], m_low[...]
            )

        copy(
            sums.at[levels, pl.ds(0, piece)], landed,
            send_sem.at[levels + 1, 0], misc_sem.at[2], partner,
        ).start()
        o_ref[0] = sums[levels, pl.ds(piece, piece)]

        for stage in range(levels):
            @pl.when(row >= 2**stage)
            def _(stage=stage):
                wait_sent(stage, 14, 15)

        for stage in range(1, levels + 1):
            @pl.when(row + 2 ** (stage - 1) <= rows_total)
            def _(stage=stage):
                wait_sent(stage, *range(6))

        wait_sent(begin, *range(9))
        wait_sent(levels + 1, 0)


def on_device(rows_total, diag_tiles, sub_tiles, boundary):
    size = diag_tiles.shape[-1]
    levels = rows_total.bit_length() - 1
    piece = size // 8
    block = size // 4
    return pl.pallas_call(
        functools.partial(kernel, rows_total, levels),
        out_shape=jax.ShapeDtypeStruct(diag_tiles.shape, F32),
        in_specs=[pl.BlockSpec(memory_space=pltpu.VMEM)] * 3,
        out_specs=pl.BlockSpec(memory_space=pltpu.VMEM),
        scratch_shapes=[
            pltpu.VMEM((2 * levels + 3, size, size), F32),
            pltpu.VMEM((levels + 1, block, size), F32),
            pltpu.VMEM((levels + 1, block, size), F32),
            pltpu.VMEM((block, size), F32),
            pltpu.VMEM((piece, size), F32),
            pltpu.VMEM((size, size), BF16),
            pltpu.VMEM((size, size), BF16),
            pltpu.VMEM((block, size), BF16),
            pltpu.VMEM((block, size), BF16),
            pltpu.SemaphoreType.DMA((2 * levels + 3, 8)),
            pltpu.SemaphoreType.DMA((levels + 1, 2)),
            pltpu.SemaphoreType.DMA((3,)),
            pltpu.SemaphoreType.DMA((levels + 3, 16)),
        ],
        compiler_params=pltpu.CompilerParams(
            collective_id=0, has_side_effects=True, vmem_limit_bytes=48 * 1024 * 1024
        ),
    )(diag_tiles, sub_tiles, boundary)


def solution(mesh):
    spec = jax.sharding.PartitionSpec
    tiles = spec("row", "col", None)
    return jax.shard_map(
        functools.partial(on_device, mesh.shape["row"]),
        mesh=mesh,
        in_specs=(tiles, tiles, spec("col", None)),
        out_specs=tiles,
        check_vma=False,
    )
```

time: 392 us -> 110 us (0.28)
  waiting for transfers between devices: 247 us -> 0 us
  matrix products: 117 us -> 0 us
  Pallas kernels: 0 us -> 106 us
  between operations: 13.9 us -> 0.01 us
  other arithmetic: 6.09 us -> 0 us
    all_gather x5 -> x0, waiting for transfers between devices: 247 us -> none  [the longest x4 211 us: prefix_by_axis(): pieces = jax.tree.map(lambda part: lax.all_gather(part, axis), so_far)]
    dot_general x46 -> x0, matrix products: 117 us -> none  [the longest x44 108 us: product(): return jnp.dot(left, right, precision=lax.Precision.HIGHEST)]
    pallas_call x0 -> x1, Pallas kernels: none -> 106 us  [on_device(): pl.pallas_call(functools.partial(kernel, rows_total, levels), out_shape=j...]
    another operation x3 -> x0, other arithmetic: 4.27 us -> none
  transfers between devices with their start and end apart: 5 -> 0, of which waited for: 5 -> 0; matrix products, arithmetic and copies ran while one was open for 20% -> 0% of each run, Pallas kernels for 0% -> 0%
where the time goes in v1:
time: 110 us; the launch traced here: 109 us
  Pallas kernels  106 us (96%)
  local copies, waits for them, and re-layouts  3.37 us (3%)
    pallas_call x1, Pallas kernels, on_device(): pl.pallas_call(functools.partial(kernel, rows_total, levels), out_shape=j...  106 us
    unnamed x7, local copies, waits for them, and re-layouts  3.37 us

profile of v1, /device:TPU:1, one launch (start us, length us, event | category | flops | bytes accessed | tf_op | source)
XLA Modules:
  0.0 109.2 jit_solution(1610178356125786835)
XLA Ops:
  0.0 0.0 copy-start
  0.0 0.9 copy-done
  0.9 0.0 copy-start.1
  0.9 0.9 copy-done.1
  1.8 0.0 copy-start.2
  1.8 0.9 copy-done.2
  2.7 105.9 %shard_map.37 = f32[1,64,512]{2,1,0:T(8,128)S(1)} custom-call(f32[1,64,512]{2,1,0:T(8,128)S(1)} %copy-done, f32[1,64,512]{2,1,0:T(8,128)S(1)} %copy-done.1, f32[64,512]{1,0:T(8,128)S(1)} %copy-done.2), custom_call_target="tpu_custom_call" | custom-call | tf_op jit(solution)/shard_map/pallas_call | solution.py:321
  108.6 0.7 copy.5
Async XLA Ops:
  0.0 0.9 copy-start
  0.9 0.9 copy-start.1
  1.8 0.9 copy-start.2

commit v2 on v0

v2 whole, which is shorter than its diff:
```python
import functools

import jax
import jax.numpy as jnp
from jax import lax
from jax.experimental import pallas as pl
from jax.experimental.pallas import tpu as pltpu

MESH = pl.DeviceIdType.MESH
BF16 = jnp.bfloat16
F32 = jnp.float32


def split(value):
    high = value.astype(BF16)
    low = (value - high.astype(F32)).astype(BF16)
    return high, low


def dot(left, right):
    return jnp.dot(left, right, preferred_element_type=F32)


def product3(left_high, left_low, right_high, right_low):
    rows = left_high.shape[0]
    both = dot(jnp.concatenate([left_high, left_low], axis=0), right_high)
    return both[:rows] + both[rows:] + dot(left_high, right_low)


def kernel(
    rows_total, levels, d_ref, s_ref, b_ref, o_ref,
    full, sums, landed, m_high, m_low, t_high, t_low,
    full_sem, misc_sem, send_sem,
):
    maps_end = levels
    s_array = 2 * levels + 1
    b_array = 2 * levels + 2
    size = d_ref.shape[-1]
    chunk = size // 8
    block = size // 4
    piece = size // 16
    row = lax.axis_index("row")
    col = lax.axis_index("col")
    ring = col // 2
    core = col % 2
    right = (ring + 1) % 4
    left = (ring + 3) % 4
    across = (ring + 2) % 4
    partner = (row, 2 * ring + (1 - core))
    to_right = (row, 2 * right + core)
    to_left = (row, 2 * left + core)
    last = rows_total - 1

    def rows_of(number, length):
        return pl.ds(pl.multiple_of(number * length, length), length)

    def part(array, number):
        return full.at[array, rows_of(number, piece)]

    def copy(src, dst, send, recv, device):
        return pltpu.make_async_remote_copy(
            src_ref=src, dst_ref=dst, send_sem=send, recv_sem=recv,
            device_id=device, device_id_type=MESH,
        )

    some = full.at[0, pl.ds(0, piece)]

    def wait_sent(stage, numbers):
        for number in numbers:
            copy(some, some, send_sem.at[stage, number], misc_sem.at[0], partner).wait_send()

    def wait_part(array, number):
        here = part(array, number)
        copy(here, here, send_sem.at[0, 0], full_sem.at[array, number], partner).wait_recv()

    def send_part(array, number, device, stage, sem):
        here = part(array, number)
        copy(here, here, send_sem.at[stage, sem], full_sem.at[array, number], device).start()

    mine = 2 * ring + core
    own_rows = rows_of(mine, chunk)
    fetches = [
        pltpu.make_async_copy(ref, full.at[array, own_rows], misc_sem.at[1 + k])
        for k, (ref, array) in enumerate(
            ((d_ref.at[0], 0), (s_ref.at[0], s_array), (b_ref, b_array))
        )
    ]
    for fetch in fetches:
        fetch.start()

    barrier = pltpu.get_barrier_semaphore()
    greeted = [partner, to_right, to_left]
    for level in range(levels):
        step = 2**level
        greeted.append(((row + step) % rows_total, col))
        greeted.append(((row + rows_total - step) % rows_total, col))
    for device in greeted:
        pl.semaphore_signal(barrier, inc=1, device_id=device, device_id_type=MESH)
    for fetch in fetches:
        fetch.wait()
    pl.semaphore_wait(barrier, len(greeted))

    def number_of(place, half):
        return 4 * place + 2 * core + half

    def gather_own(array, stage):
        for half in range(2):
            send_part(array, number_of(ring, half), to_right, stage, half)
            send_part(array, number_of(ring, 1 - half), to_left, stage, 2 + half)
        for half in range(2):
            send_part(array, number_of(ring, half), partner, stage, 4 + half)

    def gather_near(array, stage):
        wait_part(array, number_of(left, 0))
        send_part(array, number_of(left, 0), to_right, stage, 6)
        wait_part(array, number_of(right, 1))
        send_part(array, number_of(right, 1), to_left, stage, 7)
        send_part(array, number_of(left, 0), partner, stage, 8)
        send_part(array, number_of(right, 1), partner, stage, 9)
        wait_part(array, number_of(left, 1))
        send_part(array, number_of(left, 1), partner, stage, 10)
        wait_part(array, number_of(right, 0))
        send_part(array, number_of(right, 0), partner, stage, 11)

    def gather_far(array, stage):
        for half in range(2):
            wait_part(array, number_of(across, half))
            send_part(array, number_of(across, half), partner, stage, 12 + half)

    def gather_partner(array):
        for place in (ring, left, right, across):
            for half in range(2):
                wait_part(array, 4 * place + 2 * (1 - core) + half)

    at_d, at_s, at_b = levels + 1, levels + 2, levels + 3
    gather_own(0, at_d)
    gather_near(0, at_d)
    gather_own(s_array, at_s)
    gather_far(0, at_d)
    gather_near(s_array, at_s)

    @pl.when(row == last)
    def _():
        gather_own(b_array, at_b)

    gather_partner(0)

    def split_full(array):
        for place in range(4):
            rows = pl.ds(place * block, block)
            m_high[rows], m_low[rows] = split(full[array, rows])

    def split_turned(array):
        columns = rows_of(ring, block)
        t_high[...], t_low[...] = split(full[array, :, columns].T)

    def times_full(value):
        high, low = split(value)
        return product3(high, low, m_high[...], m_low[...])

    def weight_rows(place):
        rows = rows_of(place, block)
        full[1, rows] = times_full(full[s_array, rows])

    def rest_of_weight():
        gather_far(s_array, at_s)
        gather_partner(s_array)

        @pl.when(row == last)
        def _():
            gather_near(b_array, at_b)
            gather_far(b_array, at_b)
            gather_partner(b_array)

    split_full(0)

    @pl.when(core == 0)
    def _():
        def pass_map(stage):
            @pl.when(row >= 2**stage)
            def _():
                for quarter in range(4):
                    number = 4 * ring + quarter
                    copy(
                        part(stage + 1, number), part(maps_end + stage + 1, number),
                        send_sem.at[stage, quarter], full_sem.at[maps_end + stage + 1, number],
                        (row - 2**stage, col),
                    ).start()

        @pl.when(row < last)
        def _():
            for half in range(2):
                wait_part(s_array, 4 * ring + 2 + half)
            weight_rows(ring)
            pass_map(0)

        gather_far(s_array, at_s)
        for place in (left, right, across):
            for half in range(2):
                wait_part(s_array, 4 * place + 2 + half)

        @pl.when(row == last)
        def _():
            for half in range(2):
                wait_part(s_array, 4 * ring + 2 + half)
            gather_near(b_array, at_b)
            gather_far(b_array, at_b)
            gather_partner(b_array)

        @pl.when(row < last)
        def _():
            for place in (left, right, across):
                weight_rows(place)

        for stage in range(1, levels):
            @pl.when(row + 2**stage < rows_total)
            def _(stage=stage):
                array = stage + 1
                split_full(stage)
                for quarter in range(4):
                    wait_part(maps_end + stage, 4 * ring + quarter)
                rows = rows_of(ring, block)
                full[array, rows] = times_full(full[maps_end + stage, rows])
                for slot, (one, other) in enumerate(((0, 1), (2, 3), (1, 0), (3, 2))):
                    send_part(array, 4 * ring + one, to_right, stage, 4 + slot)
                    send_part(array, 4 * ring + other, to_left, stage, 8 + slot)
                if stage < levels - 1:
                    pass_map(stage)
                for quarter in range(4):
                    send_part(array, 4 * ring + quarter, partner, stage, 12 + quarter)
                for slot, quarter in enumerate((0, 2)):
                    wait_part(array, 4 * left + quarter)
                    send_part(array, 4 * left + quarter, to_right, stage, 16 + slot)
                    wait_part(array, 4 * right + quarter + 1)
                    send_part(array, 4 * right + quarter + 1, to_left, stage, 18 + slot)
                    send_part(array, 4 * left + quarter, partner, stage, 20 + slot)
                    send_part(array, 4 * right + quarter + 1, partner, stage, 22 + slot)
                for slot, quarter in enumerate((0, 2)):
                    wait_part(array, 4 * left + quarter + 1)
                    send_part(array, 4 * left + quarter + 1, partner, stage, 24 + slot)
                    wait_part(array, 4 * right + quarter)
                    send_part(array, 4 * right + quarter, partner, stage, 26 + slot)
                for quarter in range(4):
                    wait_part(array, 4 * across + quarter)
                    send_part(array, 4 * across + quarter, partner, stage, 28 + quarter)

        @pl.when((row < last) & (row >= 1))
        def _():
            wait_sent(0, range(4))

        for stage in range(1, levels):
            @pl.when(row + 2**stage < rows_total)
            def _(stage=stage):
                wait_sent(stage, range(4, 32))
                if stage < levels - 1:
                    @pl.when(row >= 2**stage)
                    def _():
                        wait_sent(stage, range(4))

        copy(landed, landed, send_sem.at[0, 0], misc_sem.at[0], partner).wait_recv()
        o_ref[0] = landed[...]

    @pl.when(core == 1)
    def _():
        def pass_sum(stage):
            @pl.when(row >= 2**stage)
            def _():
                for quarter in range(4):
                    copy(
                        sums.at[stage, pl.ds(quarter * piece, piece)],
                        part(maps_end + stage + 1, 4 * ring + quarter),
                        send_sem.at[stage, 12 + quarter],
                        full_sem.at[maps_end + stage + 1, 4 * ring + quarter],
                        (row - 2**stage, col),
                    ).start()

        def term(array, place):
            rows = rows_of(place, block)
            high, low = split(full[array, rows])
            return product3(t_high[:, rows], t_low[:, rows], high, low)

        split_turned(0)
        sums[0] = product3(t_high[...], t_low[...], m_high[...], m_low[...])

        @pl.when(row < last)
        def _():
            pass_sum(0)

        rest_of_weight()
        for place in range(4):
            weight_rows(place)
        split_full(1)
        split_turned(1)

        @pl.when(row == last)
        def _():
            total = term(b_array, 0) + term(b_array, 1) + term(b_array, 2) + term(b_array, 3)
            sums[0] = sums[0] + times_full(total)
            pass_sum(0)

        for stage in range(1, levels + 1):
            step = 2 ** (stage - 1)
            array = maps_end + stage

            @pl.when(row + step < rows_total)
            def _(stage=stage, step=step, array=array):
                if stage > 1:
                    for number in range(16):
                        wait_part(stage, number)
                    split_full(stage)
                    split_turned(stage)
                for quarter in range(4):
                    wait_part(array, 4 * ring + quarter)
                    send_part(array, 4 * ring + quarter, to_right, stage, quarter)
                    send_part(array, 4 * ring + quarter, to_left, stage, 4 + quarter)
                total = term(array, ring)
                for slot, quarter in enumerate((0, 2)):
                    wait_part(array, 4 * left + quarter)
                    send_part(array, 4 * left + quarter, to_right, stage, 8 + slot)
                    wait_part(array, 4 * right + quarter)
                    wait_part(array, 4 * left + quarter + 1)
                    wait_part(array, 4 * right + quarter + 1)
                    send_part(array, 4 * right + quarter + 1, to_left, stage, 10 + slot)
                total = total + term(array, left) + term(array, right)
                for quarter in range(4):
                    wait_part(array, 4 * across + quarter)
                total = total + term(array, across)
                sums[stage] = sums[stage - 1] + times_full(total)

            @pl.when(row + step >= rows_total)
            def _(stage=stage):
                sums[stage] = sums[stage - 1]

            if stage < levels:
                pass_sum(stage)

        for half in range(2):
            copy(
                sums.at[levels, pl.ds(half * piece, piece)],
                landed.at[pl.ds(half * piece, piece)],
                send_sem.at[0, half], misc_sem.at[0], partner,
            ).start()
        o_ref[0] = sums[levels, pl.ds(chunk, chunk)]

        for stage in range(levels):
            @pl.when(row >= 2**stage)
            def _(stage=stage):
                wait_sent(stage, range(12, 16))

        for stage in range(1, levels + 1):
            @pl.when(row + 2 ** (stage - 1) < rows_total)
            def _(stage=stage):
                wait_sent(stage, range(12))

        wait_sent(0, range(2))

    wait_sent(at_d, range(14))
    wait_sent(at_s, range(14))

    @pl.when(row == last)
    def _():
        wait_sent(at_b, range(14))


def on_device(rows_total, diag_tiles, sub_tiles, boundary):
    size = diag_tiles.shape[-1]
    levels = rows_total.bit_length() - 1
    chunk = size // 8
    block = size // 4
    arrays = 2 * levels + 3
    return pl.pallas_call(
        functools.partial(kernel, rows_total, levels),
        out_shape=jax.ShapeDtypeStruct(diag_tiles.shape, F32),
        in_specs=[pl.BlockSpec(memory_space=pl.ANY)] * 3,
        out_specs=pl.BlockSpec(memory_space=pltpu.VMEM),
        scratch_shapes=[
            pltpu.VMEM((arrays, size, size), F32),
            pltpu.VMEM((levels + 1, block, size), F32),
            pltpu.VMEM((chunk, size), F32),
            pltpu.VMEM((size, size), BF16),
            pltpu.VMEM((size, size), BF16),
            pltpu.VMEM((block, size), BF16),
            pltpu.VMEM((block, size), BF16),
            pltpu.SemaphoreType.DMA((arrays, 16)),
            pltpu.SemaphoreType.DMA((4,)),
            pltpu.SemaphoreType.DMA((levels + 4, 32)),
        ],
        compiler_params=pltpu.CompilerParams(
            collective_id=0, has_side_effects=True, vmem_limit_bytes=60 * 1024 * 1024
        ),
    )(diag_tiles, sub_tiles, boundary)


def solution(mesh):
    spec = jax.sharding.PartitionSpec
    tiles = spec("row", "col", None)
    return jax.shard_map(
        functools.partial(on_device, mesh.shape["row"]),
        mesh=mesh,
        in_specs=(tiles, tiles, spec("col", None)),
        out_specs=tiles,
        check_vma=False,
    )
```

time: 392 us -> 102 us (0.26)
  waiting for transfers between devices: 247 us -> 0 us
  matrix products: 117 us -> 0 us
  Pallas kernels: 0 us -> 100 us
  between operations: 13.9 us -> 0.01 us
  other arithmetic: 6.09 us -> 0 us
    all_gather x5 -> x0, waiting for transfers between devices: 247 us -> none  [the longest x4 211 us: prefix_by_axis(): pieces = jax.tree.map(lambda part: lax.all_gather(part, axis), so_far)]
    dot_general x46 -> x0, matrix products: 117 us -> none  [the longest x44 108 us: product(): return jnp.dot(left, right, precision=lax.Precision.HIGHEST)]
    pallas_call x0 -> x1, Pallas kernels: none -> 100 us  [on_device(): pl.pallas_call(functools.partial(kernel, rows_total, levels), out_shape=j...]
    another operation x3 -> x0, other arithmetic: 4.27 us -> none
  transfers between devices with their start and end apart: 5 -> 0, of which waited for: 5 -> 0; matrix products, arithmetic and copies ran while one was open for 20% -> 0% of each run, Pallas kernels for 0% -> 0%
where the time goes in v2:
time: 102 us
  Pallas kernels  100 us (98%)
  local copies, waits for them, and re-layouts  1.57 us (2%)
    pallas_call x1, Pallas kernels, on_device(): pl.pallas_call(functools.partial(kernel, rows_total, levels), out_shape=j...  100 us

profile of v2, /device:TPU:1, one launch (start us, length us, event | category | flops | bytes accessed | tf_op | source)
XLA Modules:
  0.0 101.5 jit_solution(9911761821353440031)
XLA Ops:
  0.0 100.0 %shard_map.37 = f32[1,64,512]{2,1,0:T(8,128)} custom-call(f32[1,64,512]{2,1,0:T(8,128)} %d_ref.1, f32[1,64,512]{2,1,0:T(8,128)} %s_ref.1, f32[64,512]{1,0:T(8,128)} %b_ref.1), custom_call_target="tpu_custom_call" | custom-call | tf_op jit(solution)/shard_map/pallas_call | solution.py:371
  100.0 1.6 %copy.5 = f32[1,64,512]{2,1,0:T(8,128)} copy(f32[1,64,512]{2,1,0:T(8,128)} %shard_map.37) | data formatting | bytes 262144

commit v3 on v2

v3 whole, which is shorter than its diff:
```python
import functools

import jax
import jax.numpy as jnp
from jax import lax
from jax.experimental import pallas as pl
from jax.experimental.pallas import tpu as pltpu

MESH = pl.DeviceIdType.MESH
BF16 = jnp.bfloat16
F32 = jnp.float32


def split(value):
    high = value.astype(BF16)
    low = (value - high.astype(F32)).astype(BF16)
    return high, low


def dot(left, right):
    return jnp.dot(left, right, preferred_element_type=F32)


def product3(left_high, left_low, right_high, right_low):
    rows = left_high.shape[0]
    both = dot(jnp.concatenate([left_high, left_low], axis=0), right_high)
    return both[:rows] + both[rows:] + dot(left_high, right_low)


def kernel(
    rows_total, levels, d_ref, s_ref, b_ref, o_ref,
    full, sums, m_high, m_low, t_high, t_low, a_high, a_low,
    input_sem, ring_sem, entry_sem, map_sem, misc_sem, send_sem,
):
    maps_end = levels
    s_array = 2 * levels + 1
    b_array = 2 * levels + 2
    size = d_ref.shape[-1]
    chunk = size // 8
    block = size // 4
    piece = size // 16
    row = lax.axis_index("row")
    col = lax.axis_index("col")
    ring = col // 2
    core = col % 2
    right = (ring + 1) % 4
    left = (ring + 3) % 4
    across = (ring + 2) % 4
    partner = (row, 2 * ring + (1 - core))
    to_right = (row, 2 * right + core)
    to_left = (row, 2 * left + core)
    last = rows_total - 1

    def rows_of(number, length):
        return pl.ds(pl.multiple_of(number * length, length), length)

    def copy(src, dst, send, recv, device):
        return pltpu.make_async_remote_copy(
            src_ref=src, dst_ref=dst, send_sem=send, recv_sem=recv,
            device_id=device, device_id_type=MESH,
        )

    def wait_for(ref, sem):
        copy(ref, ref, send_sem.at[0, 0], sem, partner).wait_recv()

    def wait_sent(sem, arrays, rows):
        some = full.at[pl.ds(0, arrays), pl.ds(0, rows)]
        copy(some, some, sem, misc_sem.at[0], partner).wait_send()

    mine = 2 * ring + core
    own_rows = rows_of(mine, chunk)
    inputs = ((d_ref.at[0], 0), (s_ref.at[0], s_array), (b_ref, b_array))
    fetches = [
        pltpu.make_async_copy(ref, full.at[array, own_rows], misc_sem.at[1 + k])
        for k, (ref, array) in enumerate(inputs)
    ]
    for fetch in fetches:
        fetch.start()

    barrier = pltpu.get_barrier_semaphore()
    greeted = [partner, to_right, to_left]
    for level in range(levels):
        step = 2**level
        greeted.append(((row + step) % rows_total, col))
        greeted.append(((row + rows_total - step) % rows_total, col))
    for device in greeted:
        pl.semaphore_signal(barrier, inc=1, device_id=device, device_id_type=MESH)
    for fetch in fetches:
        fetch.wait()
    pl.semaphore_wait(barrier, len(greeted))

    def half_of(kind, place, half):
        return full.at[inputs[kind][1], rows_of(4 * place + 2 * core + half, piece)]

    def send_half(kind, place, half, device, slot):
        here = half_of(kind, place, half)
        copy(here, here, send_sem.at[levels + 1 + kind, 0], input_sem.at[kind, slot], device).start()

    def wait_half(kind, place, half, slot):
        wait_for(half_of(kind, place, half), input_sem.at[kind, slot])

    def gather_own(kind):
        for half in range(2):
            send_half(kind, ring, half, to_right, half)
            send_half(kind, ring, 1 - half, to_left, 2 + 1 - half)
        here = full.at[inputs[kind][1], own_rows]
        copy(here, here, send_sem.at[levels + 1 + kind, 0], input_sem.at[kind, 6], partner).start()

    def gather_near(kind):
        wait_half(kind, left, 0, 0)
        send_half(kind, left, 0, to_right, 4)
        wait_half(kind, right, 1, 3)
        send_half(kind, right, 1, to_left, 5)
        send_half(kind, left, 0, partner, 7)
        send_half(kind, right, 1, partner, 7)
        wait_half(kind, left, 1, 1)
        send_half(kind, left, 1, partner, 7)
        wait_half(kind, right, 0, 2)
        send_half(kind, right, 0, partner, 7)

    def gather_far(kind):
        for half in range(2):
            wait_half(kind, across, half, 4 + half)
            send_half(kind, across, half, partner, 7)

    def gather_beside(kind):
        wait_for(full.at[0, pl.ds(0, chunk)], input_sem.at[kind, 6])

    def gather_others(kind):
        wait_for(full.at[0, pl.ds(0, 3 * chunk)], input_sem.at[kind, 7])

    gather_own(0)
    gather_near(0)
    gather_own(1)
    gather_far(0)
    gather_near(1)

    @pl.when(row == last)
    def _():
        gather_own(2)

    gather_beside(0)
    gather_others(0)

    def split_full(array):
        for place in range(4):
            rows = pl.ds(place * block, block)
            m_high[rows], m_low[rows] = split(full[array, rows])

    def split_turned(array):
        t_high[...], t_low[...] = split(full[array, :, rows_of(ring, block)].T)

    def times_full(value):
        high, low = split(value)
        return product3(high, low, m_high[...], m_low[...])

    def weight_rows(place):
        rows = rows_of(place, block)
        full[1, rows] = times_full(full[s_array, rows])

    split_full(0)

    @pl.when(core == 0)
    def _():
        def quarter_of(array, place, quarter):
            return full.at[array, rows_of(4 * place + quarter, piece)]

        def pass_map(stage):
            @pl.when(row >= 2**stage)
            def _():
                for quarter in range(4):
                    copy(
                        quarter_of(stage + 1, ring, quarter),
                        quarter_of(maps_end + stage + 1, ring, quarter),
                        send_sem.at[stage, 1], entry_sem.at[stage + 1, quarter],
                        (row - 2**stage, col),
                    ).start()

        gather_beside(1)

        @pl.when(row < last)
        def _():
            weight_rows(ring)
            pass_map(0)

        gather_far(1)

        @pl.when(row == last)
        def _():
            gather_near(2)
            gather_far(2)
            gather_beside(2)
            gather_others(2)

        gather_others(1)

        @pl.when(row < last)
        def _():
            for place in (left, right, across):
                weight_rows(place)

        for stage in range(1, levels):
            @pl.when(row + 2**stage < rows_total)
            def _(stage=stage):
                array = stage + 1

                def send(place, quarter, device, slot):
                    here = quarter_of(array, place, quarter)
                    copy(
                        here, here, send_sem.at[stage, 0], ring_sem.at[stage % 2, slot], device
                    ).start()

                def hand_over(place, quarter):
                    here = quarter_of(array, place, quarter)
                    copy(here, here, send_sem.at[stage, 2], map_sem.at[stage], partner).start()

                def wait(place, quarter, slot):
                    wait_for(quarter_of(array, place, quarter), ring_sem.at[stage % 2, slot])

                split_full(stage)
                for quarter in range(4):
                    wait_for(
                        quarter_of(maps_end + stage, ring, quarter), entry_sem.at[stage, quarter]
                    )
                rows = rows_of(ring, block)
                full[array, rows] = times_full(full[maps_end + stage, rows])
                for one, other in ((0, 1), (2, 3), (1, 0), (3, 2)):
                    send(ring, one, to_right, one)
                    send(ring, other, to_left, 4 + other)
                if stage < levels - 1:
                    pass_map(stage)
                for quarter in range(4):
                    hand_over(ring, quarter)
                for quarter in (0, 2):
                    wait(left, quarter, quarter)
                    send(left, quarter, to_right, 8 + quarter)
                    wait(right, quarter + 1, 5 + quarter)
                    send(right, quarter + 1, to_left, 9 + quarter)
                    hand_over(left, quarter)
                    hand_over(right, quarter + 1)
                for quarter in (0, 2):
                    wait(left, quarter + 1, quarter + 1)
                    hand_over(left, quarter + 1)
                    wait(right, quarter, 4 + quarter)
                    hand_over(right, quarter)
                for quarter in range(4):
                    wait(across, quarter, 8 + quarter)
                    hand_over(across, quarter)

        @pl.when((row < last) & (row >= 1))
        def _():
            wait_sent(send_sem.at[0, 1], 1, block)

        for stage in range(1, levels):
            @pl.when(row + 2**stage < rows_total)
            def _(stage=stage):
                wait_sent(send_sem.at[stage, 0], 3, block)
                wait_sent(send_sem.at[stage, 2], 1, size)
                if stage < levels - 1:
                    @pl.when(row >= 2**stage)
                    def _():
                        wait_sent(send_sem.at[stage, 1], 1, block)

        wait_for(o_ref.at[0], misc_sem.at[0])

    @pl.when(core == 1)
    def _():
        def block_of(array, place, number, half=None):
            rows = rows_of(place, block) if half is None else rows_of(2 * place + half, chunk)
            return array, rows, rows_of((place + number) % 4, block)

        def if_sent(place, number, act):
            if number < 2:
                act()
            else:
                pl.when(place < 2)(act)

        def pass_sum(stage):
            target = maps_end + stage + 1

            @pl.when(row >= 2**stage)
            def _():
                for number in range(3):
                    @functools.partial(if_sent, ring, number)
                    def _(number=number):
                        for half in range(2):
                            there = block_of(target, ring, number, half)
                            copy(
                                sums.at[stage, pl.ds(half * chunk, chunk), there[2]],
                                full.at[there],
                                send_sem.at[stage, 1], entry_sem.at[stage + 1, 2 * number + half],
                                (row - 2**stage, col),
                            ).start()

        def put(array, place, number):
            there = block_of(array, place, number)
            value = full[there]
            a_high[there[1:]], a_low[there[1:]] = split(value)
            if number:
                turned = (there[2], there[1])
                a_high[turned], a_low[turned] = split(value.T)

        def compose(before):
            inner = product3(t_high[...], t_low[...], a_high[...], a_low[...])
            return before + times_full(inner)

        split_turned(0)
        sums[0] = product3(t_high[...], t_low[...], m_high[...], m_low[...])

        @pl.when(row < last)
        def _():
            pass_sum(0)

        gather_far(1)
        gather_beside(1)
        gather_others(1)

        @pl.when(row == last)
        def _():
            gather_near(2)

        for place in range(4):
            weight_rows(place)
        split_full(1)
        split_turned(1)

        @pl.when(row == last)
        def _():
            gather_far(2)
            gather_beside(2)
            gather_others(2)
            for place in range(4):
                rows = pl.ds(place * block, block)
                a_high[rows], a_low[rows] = split(full[b_array, rows])
            sums[0] = compose(sums[0])
            pass_sum(0)

        for stage in range(1, levels + 1):
            step = 2 ** (stage - 1)
            array = maps_end + stage

            @pl.when(row + step < rows_total)
            def _(stage=stage, step=step, array=array):
                def send(place, number, half, device, slot):
                    here = full.at[block_of(array, place, number, half)]
                    copy(
                        here, here, send_sem.at[stage, 0],
                        ring_sem.at[stage % 2, slot + 2 * number + half], device,
                    ).start()

                def wait(place, number, half, slot):
                    here = full.at[block_of(array, place, number, half)]
                    wait_for(here, ring_sem.at[stage % 2, slot + 2 * number + half])

                if stage > 1:
                    wait_for(full.at[stage], map_sem.at[stage - 1])
                    split_full(stage)
                    split_turned(stage)
                for number in range(3):
                    @functools.partial(if_sent, ring, number)
                    def _(number=number):
                        for half in range(2):
                            here = full.at[block_of(array, ring, number, half)]
                            wait_for(here, entry_sem.at[stage, 2 * number + half])
                            send(ring, number, half, to_right, 0)
                            send(ring, number, half, to_left, 6)
                for number in range(3):
                    if_sent(ring, number, functools.partial(put, array, ring, number))
                for number in range(3):
                    @functools.partial(if_sent, left, number)
                    def _(number=number):
                        wait(left, number, 0, 0)
                        send(left, number, 0, to_right, 12)

                    @functools.partial(if_sent, right, number)
                    def _(number=number):
                        wait(right, number, 1, 6)
                        send(right, number, 1, to_left, 12)
                for number in range(3):
                    @functools.partial(if_sent, left, number)
                    def _(number=number):
                        wait(left, number, 1, 0)
                        put(array, left, number)

                    @functools.partial(if_sent, right, number)
                    def _(number=number):
                        wait(right, number, 0, 6)
                        put(array, right, number)
                for number in range(3):
                    @functools.partial(if_sent, across, number)
                    def _(number=number):
                        wait(across, number, 0, 12)
                        wait(across, number, 1, 12)
                        put(array, across, number)
                sums[stage] = compose(sums[stage - 1])

            @pl.when(row + step >= rows_total)
            def _(stage=stage):
                sums[stage] = sums[stage - 1]

            if stage < levels:
                pass_sum(stage)

        upper = copy(
            sums.at[levels, pl.ds(0, chunk)], o_ref.at[0],
            send_sem.at[0, 0], misc_sem.at[0], partner,
        )
        lower = pltpu.make_async_copy(
            sums.at[levels, pl.ds(chunk, chunk)], o_ref.at[0], misc_sem.at[1]
        )
        upper.start()
        lower.start()

        def wait_blocks(sem, first, others):
            @pl.when(ring < 2)
            def _():
                wait_sent(sem, 1, first * piece // 2)

            @pl.when(ring >= 2)
            def _():
                wait_sent(sem, 1, others * piece // 2)

        for stage in range(levels):
            @pl.when(row >= 2**stage)
            def _(stage=stage):
                wait_blocks(send_sem.at[stage, 1], 6, 4)

        for stage in range(1, levels + 1):
            @pl.when(row + 2 ** (stage - 1) < rows_total)
            def _(stage=stage):
                wait_blocks(send_sem.at[stage, 0], 17, 13)

        lower.wait()
        upper.wait_send()

    for kind in range(2):
        wait_sent(send_sem.at[levels + 1 + kind, 0], 1, 7 * chunk)

    @pl.when(row == last)
    def _():
        wait_sent(send_sem.at[levels + 3, 0], 1, 7 * chunk)


def on_device(rows_total, diag_tiles, sub_tiles, boundary):
    size = diag_tiles.shape[-1]
    levels = rows_total.bit_length() - 1
    block = size // 4
    arrays = 2 * levels + 3
    return pl.pallas_call(
        functools.partial(kernel, rows_total, levels),
        out_shape=jax.ShapeDtypeStruct(diag_tiles.shape, F32),
        in_specs=[pl.BlockSpec(memory_space=pl.ANY)] * 3,
        out_specs=pl.BlockSpec(memory_space=pl.ANY),
        scratch_shapes=[
            pltpu.VMEM((arrays, size, size), F32),
            pltpu.VMEM((levels + 1, block, size), F32),
            pltpu.VMEM((size, size), BF16),
            pltpu.VMEM((size, size), BF16),
            pltpu.VMEM((block, size), BF16),
            pltpu.VMEM((block, size), BF16),
            pltpu.VMEM((size, size), BF16),
            pltpu.VMEM((size, size), BF16),
            pltpu.SemaphoreType.DMA((3, 8)),
            pltpu.SemaphoreType.DMA((2, 18)),
            pltpu.SemaphoreType.DMA((levels + 1, 6)),
            pltpu.SemaphoreType.DMA((levels,)),
            pltpu.SemaphoreType.DMA((4,)),
            pltpu.SemaphoreType.DMA((levels + 4, 3)),
        ],
        compiler_params=pltpu.CompilerParams(
            collective_id=0, has_side_effects=True, vmem_limit_bytes=60 * 1024 * 1024
        ),
    )(diag_tiles, sub_tiles, boundary)


def solution(mesh):
    spec = jax.sharding.PartitionSpec
    tiles = spec("row", "col", None)
    return jax.shard_map(
        functools.partial(on_device, mesh.shape["row"]),
        mesh=mesh,
        in_specs=(tiles, tiles, spec("col", None)),
        out_specs=tiles,
        check_vma=False,
    )
```

time: 102 us -> 84.2 us (0.83)
  Pallas kernels: 100 us -> 82.5 us
    pallas_call x1, Pallas kernels: 100 us -> 82.5 us  [on_device(): pl.pallas_call(functools.partial(kernel, rows_total, levels), out_shape=j...]
where the time goes in v3:
time: 84.2 us; the launch traced here: 84.1 us
  Pallas kernels  82.5 us (98%)
  local copies, waits for them, and re-layouts  1.57 us (2%)
    pallas_call x1, Pallas kernels, on_device(): pl.pallas_call(functools.partial(kernel, rows_total, levels), out_shape=j...  82.5 us

profile of v3, /device:TPU:1, one launch (start us, length us, event | category | flops | bytes accessed | tf_op | source)
XLA Modules:
  0.0 84.1 jit_solution(11436289527088315726)
XLA Ops:
  0.0 82.5 %shard_map.37 = f32[1,64,512]{2,1,0:T(8,128)} custom-call(f32[1,64,512]{2,1,0:T(8,128)} %d_ref.1, f32[1,64,512]{2,1,0:T(8,128)} %s_ref.1, f32[64,512]{1,0:T(8,128)} %b_ref.1), custom_call_target="tpu_custom_call" | custom-call | tf_op jit(solution)/shard_map/pallas_call | solution.py:449
  82.5 1.6 %copy.5 = f32[1,64,512]{2,1,0:T(8,128)} copy(f32[1,64,512]{2,1,0:T(8,128)} %shard_map.37) | data formatting | bytes 262144

commit v4 on v3

v4 whole, which is shorter than its diff:
```python
import functools

import jax
import jax.numpy as jnp
from jax import lax
from jax.experimental import pallas as pl
from jax.experimental.pallas import tpu as pltpu

MESH = pl.DeviceIdType.MESH
BF16 = jnp.bfloat16
F32 = jnp.float32


def split(value):
    high = value.astype(BF16)
    low = (value - high.astype(F32)).astype(BF16)
    return high, low


def dot(left, right):
    return jnp.dot(left, right, preferred_element_type=F32)


def product3(left_high, left_low, right_high, right_low):
    rows = left_high.shape[0]
    both = dot(jnp.concatenate([left_high, left_low], axis=0), right_high)
    return both[:rows] + both[rows:] + dot(left_high, right_low)


def kernel(
    rows_total, levels, d_ref, s_ref, b_ref, o_ref,
    full, sums, halves, m_high, m_low, t_high, t_low, a_high, a_low,
    input_sem, ring_sem, entry_sem, map_sem, misc_sem, send_sem,
):
    maps_end = levels
    s_array = 2 * levels + 1
    b_array = 2 * levels + 2
    size = d_ref.shape[-1]
    chunk = size // 8
    block = size // 4
    piece = size // 16
    row = lax.axis_index("row")
    col = lax.axis_index("col")
    ring = col // 2
    core = col % 2
    right = (ring + 1) % 4
    left = (ring + 3) % 4
    across = (ring + 2) % 4
    partner = (row, 2 * ring + (1 - core))
    to_right = (row, 2 * right + core)
    to_left = (row, 2 * left + core)
    last = rows_total - 1

    def rows_of(number, length):
        return pl.ds(pl.multiple_of(number * length, length), length)

    def copy(src, dst, send, recv, device):
        return pltpu.make_async_remote_copy(
            src_ref=src, dst_ref=dst, send_sem=send, recv_sem=recv,
            device_id=device, device_id_type=MESH,
        )

    def wait_for(ref, sem):
        copy(ref, ref, send_sem.at[0, 0], sem, partner).wait_recv()

    def wait_sent(sem, arrays, rows):
        some = full.at[pl.ds(0, arrays), pl.ds(0, rows)]
        copy(some, some, sem, misc_sem.at[0], partner).wait_send()

    mine = 2 * ring + core
    own_rows = rows_of(mine, chunk)
    inputs = ((d_ref.at[0], 0), (s_ref.at[0], s_array), (b_ref, b_array))
    fetches = [
        pltpu.make_async_copy(ref, full.at[array, own_rows], misc_sem.at[1 + k])
        for k, (ref, array) in enumerate(inputs)
    ]
    for fetch in fetches:
        fetch.start()

    barrier = pltpu.get_barrier_semaphore()
    greeted = [partner, to_right, to_left]
    for level in range(levels):
        step = 2**level
        greeted.append(((row + step) % rows_total, col))
        greeted.append(((row + rows_total - step) % rows_total, col))
    for device in greeted:
        pl.semaphore_signal(barrier, inc=1, device_id=device, device_id_type=MESH)
    for fetch in fetches:
        fetch.wait()
    pl.semaphore_wait(barrier, len(greeted))

    def input_piece(kind, place, number):
        return full.at[inputs[kind][1], rows_of(4 * place + number, piece)]

    def send_input(kind, place, number, device, slot):
        here = input_piece(kind, place, number)
        copy(here, here, send_sem.at[levels + 1 + kind, 0], input_sem.at[kind, slot], device).start()

    def wait_input(kind, place, number, slot):
        wait_for(input_piece(kind, place, number), input_sem.at[kind, slot])

    def hand_own(kind):
        here = full.at[inputs[kind][1], own_rows]
        copy(here, here, send_sem.at[levels + 1 + kind, 1], input_sem.at[kind, 12], partner).start()

    def gather_own(kind, numbers):
        for number in numbers:
            send_input(kind, ring, number, to_right, number)
        for number in reversed(numbers):
            send_input(kind, ring, number, to_left, 4 + number)

    def gather_near(kind):
        for number in (2, 0):
            wait_input(kind, left, number, number)
            send_input(kind, left, number, to_right, 8 + number)
            wait_input(kind, right, number + 1, 5 + number)
            send_input(kind, right, number + 1, to_left, 9 + number)
            send_input(kind, left, number, partner, 13)
            send_input(kind, right, number + 1, partner, 13)
        for number in (2, 0):
            wait_input(kind, left, number + 1, number + 1)
            send_input(kind, left, number + 1, partner, 13)
            wait_input(kind, right, number, 4 + number)
            send_input(kind, right, number, partner, 13)

    def gather_far(kind):
        for number in (2, 3, 0, 1):
            wait_input(kind, across, number, 8 + number)
            send_input(kind, across, number, partner, 13)

    def wait_beside(kind):
        wait_for(full.at[0, pl.ds(0, chunk)], input_sem.at[kind, 12])

    def wait_others(kind):
        wait_for(full.at[0, pl.ds(0, 3 * block)], input_sem.at[kind, 13])

    def split_full(array):
        for place in range(4):
            rows = pl.ds(place * block, block)
            m_high[rows], m_low[rows] = split(full[array, rows])

    def split_turned(array):
        t_high[...], t_low[...] = split(full[array, :, rows_of(ring, block)].T)

    def times_full(value):
        high, low = split(value)
        return product3(high, low, m_high[...], m_low[...])

    def weight_rows(place):
        rows = rows_of(place, block)
        full[1, rows] = times_full(full[s_array, rows])

    @pl.when(core == 0)
    def _():
        hand_own(0)
        hand_own(1)

        @pl.when(row == last)
        def _():
            hand_own(2)

        def quarter_of(array, place, quarter):
            return full.at[array, rows_of(4 * place + quarter, piece)]

        def pass_map(stage):
            @pl.when(row >= 2**stage)
            def _():
                for quarter in range(4):
                    copy(
                        quarter_of(stage + 1, ring, quarter),
                        quarter_of(maps_end + stage + 1, ring, quarter),
                        send_sem.at[stage, 1], entry_sem.at[stage + 1, quarter],
                        (row - 2**stage, col),
                    ).start()

        wait_beside(0)
        wait_beside(1)
        wait_others(0)

        @pl.when(row < last)
        def _():
            split_full(0)
            weight_rows(ring)
            pass_map(0)

        wait_others(1)

        @pl.when(row < last)
        def _():
            for place in (left, right, across):
                weight_rows(place)

        for stage in range(1, levels):
            @pl.when(row + 2**stage < rows_total)
            def _(stage=stage):
                array = stage + 1

                def eighth_of(place, eighth):
                    return full.at[array, rows_of(8 * place + eighth, piece // 2)]

                def send(place, eighth, device, slot):
                    here = eighth_of(place, eighth)
                    copy(
                        here, here, send_sem.at[stage, 0], ring_sem.at[stage % 2, slot], device
                    ).start()

                def hand_over(place, eighth):
                    here = eighth_of(place, eighth)
                    copy(here, here, send_sem.at[stage, 2], map_sem.at[stage], partner).start()

                def wait(place, eighth, slot):
                    wait_for(eighth_of(place, eighth), ring_sem.at[stage % 2, slot])

                split_full(stage)
                for quarter in range(4):
                    wait_for(
                        quarter_of(maps_end + stage, ring, quarter), entry_sem.at[stage, quarter]
                    )
                rows = rows_of(ring, block)
                full[array, rows] = times_full(full[maps_end + stage, rows])
                for eighth in (0, 2, 4, 6, 1, 3, 5, 7):
                    other = eighth + 1 - 2 * (eighth % 2)
                    send(ring, eighth, to_right, eighth)
                    send(ring, other, to_left, 8 + other)
                if stage < levels - 1:
                    pass_map(stage)
                for eighth in range(8):
                    hand_over(ring, eighth)
                for eighth in (0, 2, 4, 6):
                    wait(left, eighth, eighth)
                    send(left, eighth, to_right, 16 + eighth)
                    wait(right, eighth + 1, 9 + eighth)
                    send(right, eighth + 1, to_left, 17 + eighth)
                    hand_over(left, eighth)
                    hand_over(right, eighth + 1)
                for eighth in (0, 2, 4, 6):
                    wait(left, eighth + 1, eighth + 1)
                    hand_over(left, eighth + 1)
                    wait(right, eighth, 8 + eighth)
                    hand_over(right, eighth)
                for eighth in range(8):
                    wait(across, eighth, 16 + eighth)
                    hand_over(across, eighth)

        @pl.when((row < last) & (row >= 1))
        def _():
            wait_sent(send_sem.at[0, 1], 1, block)

        for stage in range(1, levels):
            @pl.when(row + 2**stage < rows_total)
            def _(stage=stage):
                wait_sent(send_sem.at[stage, 0], 3, block)
                wait_sent(send_sem.at[stage, 2], 1, size)
                if stage < levels - 1:
                    @pl.when(row >= 2**stage)
                    def _():
                        wait_sent(send_sem.at[stage, 1], 1, block)

        wait_for(o_ref.at[0], misc_sem.at[0])

    @pl.when(core == 1)
    def _():
        def piece_of(array, place, number):
            if number < 4:
                first, second = 2 * place + number % 2, (place + number // 2) % 4
            else:
                first, second = 2 * (place % 2) + place // 2, place % 2 + 2
            return full.at[array, rows_of(first, chunk), rows_of(second, block)]

        def pass_sum(stage):
            target = maps_end + stage + 1

            @pl.when(row >= 2**stage)
            def _():
                def start(source, number):
                    copy(
                        source, piece_of(target, ring, number),
                        send_sem.at[stage, 1], entry_sem.at[stage + 1, number],
                        (row - 2**stage, col),
                    ).start()

                for number in range(4):
                    start(
                        sums.at[
                            stage, pl.ds(number % 2 * chunk, chunk),
                            rows_of((ring + number // 2) % 4, block),
                        ],
                        number,
                    )
                shared = sums[stage, :, rows_of(across, block)]

                @pl.when(ring < 2)
                def _():
                    halves[stage] = shared[:chunk]

                @pl.when(ring >= 2)
                def _():
                    halves[stage] = shared.T[chunk:]

                start(halves.at[stage], 4)

        def wait_passed(stage):
            @pl.when(row >= 2**stage)
            def _():
                wait_sent(send_sem.at[stage, 1], 1, 5 * piece // 2)

        def put(array, place, second, turn):
            rows, columns = rows_of(place, block), rows_of(second, block)
            value = full[array, rows, columns]
            a_high[rows, columns], a_low[rows, columns] = split(value)
            if turn:
                a_high[columns, rows], a_low[columns, rows] = split(value.T)

        def send_sum(stage, array, place, number, device, slot):
            here = piece_of(array, place, number)
            sent = send_sem.at[stage, 0] if stage <= levels else send_sem.at[levels + 1, 2]
            copy(here, here, sent, ring_sem.at[stage % 2, slot + number], device).start()

        def wait_sum(stage, array, place, number, slot):
            wait_for(piece_of(array, place, number), ring_sem.at[stage % 2, slot + number])

        def sum_own(stage, array, arrival):
            for number in range(5):
                arrival(number)
                send_sum(stage, array, ring, number, to_right, 0)
                send_sum(stage, array, ring, number, to_left, 5)
            put(array, ring, ring, False)
            put(array, ring, right, True)

        def sum_near(stage, array):
            for number in (0, 2, 4):
                wait_sum(stage, array, left, number, 0)
                send_sum(stage, array, left, number, to_right, 10)
                if number < 4:
                    wait_sum(stage, array, right, number + 1, 5)
                    send_sum(stage, array, right, number + 1, to_left, 10)
            wait_sum(stage, array, left, 1, 0)
            put(array, left, left, False)
            wait_sum(stage, array, right, 0, 5)
            put(array, right, right, False)
            wait_sum(stage, array, left, 3, 0)
            put(array, left, ring, True)
            wait_sum(stage, array, right, 2, 5)
            put(array, right, across, True)
            wait_sum(stage, array, right, 4, 5)
            put(array, left % 2, left % 2 + 2, True)

        def sum_far(stage, array):
            for number in range(5):
                wait_sum(stage, array, across, number, 10)
                if number == 1:
                    put(array, across, across, False)
                if number == 3:
                    put(array, across, left, True)
            put(array, ring % 2, ring % 2 + 2, True)

        def compose(before):
            inner = product3(t_high[...], t_low[...], a_high[...], a_low[...])
            return before + times_full(inner)

        gather_own(0, (2, 3))
        hand_own(0)
        wait_beside(0)
        gather_own(0, (0, 1))
        gather_near(0)
        hand_own(1)
        wait_beside(1)
        gather_own(1, (2, 3, 0, 1))

        @pl.when(row == last)
        def _():
            wait_beside(2)

            @pl.when(ring >= 2)
            def _():
                shared = full[b_array, rows_of(ring, block), rows_of(ring - 2, block)]
                full[b_array, rows_of(2 * (ring - 2) + 1, chunk), rows_of(ring, block)] = (
                    shared.T[chunk:]
                )

            sum_own(levels + 1, b_array, lambda number: None)

        gather_far(0)
        split_full(0)
        split_turned(0)
        sums[0] = product3(t_high[...], t_low[...], m_high[...], m_low[...])

        @pl.when(row < last)
        def _():
            pass_sum(0)

        gather_near(1)

        @pl.when(row == last)
        def _():
            sum_near(levels + 1, b_array)

        gather_far(1)
        for place in range(4):
            weight_rows(place)
        split_full(1)
        split_turned(1)

        @pl.when(row == last)
        def _():
            sum_far(levels + 1, b_array)
            sums[0] = compose(sums[0])
            pass_sum(0)

        for stage in range(1, levels + 1):
            step = 2 ** (stage - 1)
            array = maps_end + stage

            @pl.when(row + step < rows_total)
            def _(stage=stage, step=step, array=array):
                if stage > 1:
                    wait_for(full.at[stage], map_sem.at[stage - 1])
                    split_full(stage)
                    split_turned(stage)

                def arrival(number):
                    wait_for(piece_of(array, ring, number), entry_sem.at[stage, number])

                sum_own(stage, array, arrival)
                sum_near(stage, array)
                sum_far(stage, array)
                sums[stage] = compose(sums[stage - 1])

            @pl.when(row + step >= rows_total)
            def _(stage=stage):
                sums[stage] = sums[stage - 1]
                wait_passed(stage - 1)

            if stage < levels:
                pass_sum(stage)

        upper = copy(
            sums.at[levels, pl.ds(0, chunk)], o_ref.at[0],
            send_sem.at[0, 0], misc_sem.at[0], partner,
        )
        lower = pltpu.make_async_copy(
            sums.at[levels, pl.ds(chunk, chunk)], o_ref.at[0], misc_sem.at[1]
        )
        upper.start()
        lower.start()

        for stage in range(levels):
            @pl.when(row + 2**stage < rows_total)
            def _(stage=stage):
                wait_passed(stage)

        for stage in range(1, levels + 1):
            @pl.when(row + 2 ** (stage - 1) < rows_total)
            def _(stage=stage):
                wait_sent(send_sem.at[stage, 0], 1, 15 * piece // 2)

        @pl.when(row == last)
        def _():
            wait_sent(send_sem.at[levels + 1, 2], 1, 15 * piece // 2)

        for kind in range(2):
            wait_sent(send_sem.at[levels + 1 + kind, 0], 2, 12 * piece)
        lower.wait()
        upper.wait_send()

    for kind in range(2):
        wait_sent(send_sem.at[levels + 1 + kind, 1], 1, chunk)

    @pl.when((row == last) & (core == 0))
    def _():
        wait_sent(send_sem.at[levels + 3, 1], 1, chunk)


def on_device(rows_total, diag_tiles, sub_tiles, boundary):
    size = diag_tiles.shape[-1]
    levels = rows_total.bit_length() - 1
    block = size // 4
    arrays = 2 * levels + 3
    return pl.pallas_call(
        functools.partial(kernel, rows_total, levels),
        out_shape=jax.ShapeDtypeStruct(diag_tiles.shape, F32),
        in_specs=[pl.BlockSpec(memory_space=pl.ANY)] * 3,
        out_specs=pl.BlockSpec(memory_space=pl.ANY),
        scratch_shapes=[
            pltpu.VMEM((arrays, size, size), F32),
            pltpu.VMEM((levels + 1, block, size), F32),
            pltpu.VMEM((levels, size // 8, block), F32),
            pltpu.VMEM((size, size), BF16),
            pltpu.VMEM((size, size), BF16),
            pltpu.VMEM((block, size), BF16),
            pltpu.VMEM((block, size), BF16),
            pltpu.VMEM((size, size), BF16),
            pltpu.VMEM((size, size), BF16),
            pltpu.SemaphoreType.DMA((3, 14)),
            pltpu.SemaphoreType.DMA((2, 24)),
            pltpu.SemaphoreType.DMA((levels + 1, 5)),
            pltpu.SemaphoreType.DMA((levels,)),
            pltpu.SemaphoreType.DMA((4,)),
            pltpu.SemaphoreType.DMA((levels + 4, 3)),
        ],
        compiler_params=pltpu.CompilerParams(
            collective_id=0, has_side_effects=True, vmem_limit_bytes=60 * 1024 * 1024
        ),
    )(diag_tiles, sub_tiles, boundary)


def solution(mesh):
    spec = jax.sharding.PartitionSpec
    tiles = spec("row", "col", None)
    return jax.shard_map(
        functools.partial(on_device, mesh.shape["row"]),
        mesh=mesh,
        in_specs=(tiles, tiles, spec("col", None)),
        out_specs=tiles,
        check_vma=False,
    )
```

time: 84.2 us -> 79.8 us (0.948)
  Pallas kernels: 82.5 us -> 78.1 us
    pallas_call x1, Pallas kernels: 82.5 us -> 78.1 us  [on_device(): pl.pallas_call(functools.partial(kernel, rows_total, levels), out_shape=j...]
where the time goes in v4:
time: 79.8 us; the launch traced here: 79.7 us
  Pallas kernels  78.1 us (98%)
  local copies, waits for them, and re-layouts  1.57 us (2%)
    pallas_call x1, Pallas kernels, on_device(): pl.pallas_call(functools.partial(kernel, rows_total, levels), out_shape=j...  78.1 us

profile of v4, /device:TPU:1, one launch (start us, length us, event | category | flops | bytes accessed | tf_op | source)
XLA Modules:
  0.0 79.7 jit_solution(7886233295986841087)
XLA Ops:
  0.0 78.1 %shard_map.37 = f32[1,64,512]{2,1,0:T(8,128)} custom-call(f32[1,64,512]{2,1,0:T(8,128)} %d_ref.1, f32[1,64,512]{2,1,0:T(8,128)} %s_ref.1, f32[64,512]{1,0:T(8,128)} %b_ref.1), custom_call_target="tpu_custom_call" | custom-call | tf_op jit(solution)/shard_map/pallas_call | solution.py:479
  78.2 1.6 %copy.5 = f32[1,64,512]{2,1,0:T(8,128)} copy(f32[1,64,512]{2,1,0:T(8,128)} %shard_map.37) | data formatting | bytes 262144

commit v5 on v4

--- a/solution.py
+++ b/solution.py
@@ -30,7 +30,7 @@
 def kernel(
     rows_total, levels, d_ref, s_ref, b_ref, o_ref,
     full, sums, halves, m_high, m_low, t_high, t_low, a_high, a_low,
-    input_sem, ring_sem, entry_sem, map_sem, misc_sem, send_sem,
+    input_sem, ring_sem, entry_sem, map_sem, misc_sem, send_sem, known_sem,
 ):
     maps_end = levels
     s_array = 2 * levels + 1
@@ -77,17 +77,39 @@
     for fetch in fetches:
         fetch.start()
 
+    def rows_away(step):
+        return ((row + step) % rows_total, col), ((row + rows_total - step) % rows_total, col)
+
+    def tell(round):
+        for device in rows_away(2**round):
+            pl.semaphore_signal(
+                known_sem.at[round], inc=1, device_id=device, device_id_type=MESH
+            )
+
+    def know(round):
+        pl.semaphore_wait(known_sem.at[round], 2)
+        if round < levels - 2:
+            tell(round + 1)
+
     barrier = pltpu.get_barrier_semaphore()
-    greeted = [partner, to_right, to_left]
-    for level in range(levels):
-        step = 2**level
-        greeted.append(((row + step) % rows_total, col))
-        greeted.append(((row + rows_total - step) % rows_total, col))
+    greeted = (partner, to_right, to_left, *rows_away(1))
     for device in greeted:
         pl.semaphore_signal(barrier, inc=1, device_id=device, device_id_type=MESH)
     for fetch in fetches:
         fetch.wait()
     pl.semaphore_wait(barrier, len(greeted))
+    tell(0)
+
+    def near_link_last(from_left, from_right):
+        @pl.when(ring < 2)
+        def _():
+            from_right()
+            from_left()
+
+        @pl.when(ring >= 2)
+        def _():
+            from_left()
+            from_right()
 
     def input_piece(kind, place, number):
         return full.at[inputs[kind][1], rows_of(4 * place + number, piece)]
@@ -110,18 +132,21 @@
             send_input(kind, ring, number, to_left, 4 + number)
 
     def gather_near(kind):
-        for number in (2, 0):
-            wait_input(kind, left, number, number)
-            send_input(kind, left, number, to_right, 8 + number)
-            wait_input(kind, right, number + 1, 5 + number)
-            send_input(kind, right, number + 1, to_left, 9 + number)
-            send_input(kind, left, number, partner, 13)
-            send_input(kind, right, number + 1, partner, 13)
-        for number in (2, 0):
-            wait_input(kind, left, number + 1, number + 1)
-            send_input(kind, left, number + 1, partner, 13)
-            wait_input(kind, right, number, 4 + number)
-            send_input(kind, right, number, partner, 13)
+        def from_left():
+            for number in (2, 0, 3, 1):
+                wait_input(kind, left, number, number)
+                if number % 2 == 0:
+                    send_input(kind, left, number, to_right, 8 + number)
+                send_input(kind, left, number, partner, 13)
+
+        def from_right():
+            for number in (3, 1, 2, 0):
+                wait_input(kind, right, number, 4 + number)
+                if number % 2 == 1:
+                    send_input(kind, right, number, to_left, 8 + number)
+                send_input(kind, right, number, partner, 13)
+
+        near_link_last(from_left, from_right)
 
     def gather_far(kind):
         for number in (2, 3, 0, 1):
@@ -174,7 +199,9 @@
                     ).start()
 
         wait_beside(0)
+        know(0)
         wait_beside(1)
+        know(1)
         wait_others(0)
 
         @pl.when(row < last)
@@ -183,6 +210,8 @@
             weight_rows(ring)
             pass_map(0)
 
+        for round in range(2, levels - 1):
+            know(round)
         wait_others(1)
 
         @pl.when(row < last)
@@ -226,13 +255,20 @@
                     pass_map(stage)
                 for eighth in range(8):
                     hand_over(ring, eighth)
-                for eighth in (0, 2, 4, 6):
-                    wait(left, eighth, eighth)
-                    send(left, eighth, to_right, 16 + eighth)
-                    wait(right, eighth + 1, 9 + eighth)
-                    send(right, eighth + 1, to_left, 17 + eighth)
-                    hand_over(left, eighth)
-                    hand_over(right, eighth + 1)
+
+                def from_left():
+                    for eighth in (0, 2, 4, 6):
+                        wait(left, eighth, eighth)
+                        send(left, eighth, to_right, 16 + eighth)
+                        hand_over(left, eighth)
+
+                def from_right():
+                    for eighth in (1, 3, 5, 7):
+                        wait(right, eighth, 8 + eighth)
+                        send(right, eighth, to_left, 16 + eighth)
+                        hand_over(right, eighth)
+
+                near_link_last(from_left, from_right)
                 for eighth in (0, 2, 4, 6):
                     wait(left, eighth + 1, eighth + 1)
                     hand_over(left, eighth + 1)
@@ -328,12 +364,17 @@
             put(array, ring, right, True)
 
         def sum_near(stage, array):
-            for number in (0, 2, 4):
-                wait_sum(stage, array, left, number, 0)
-                send_sum(stage, array, left, number, to_right, 10)
-                if number < 4:
-                    wait_sum(stage, array, right, number + 1, 5)
-                    send_sum(stage, array, right, number + 1, to_left, 10)
+            def from_left():
+                for number in (0, 2, 4):
+                    wait_sum(stage, array, left, number, 0)
+                    send_sum(stage, array, left, number, to_right, 10)
+
+            def from_right():
+                for number in (1, 3):
+                    wait_sum(stage, array, right, number, 5)
+                    send_sum(stage, array, right, number, to_left, 10)
+
+            near_link_last(from_left, from_right)
             wait_sum(stage, array, left, 1, 0)
             put(array, left, left, False)
             wait_sum(stage, array, right, 0, 5)
@@ -380,7 +421,9 @@
 
             sum_own(levels + 1, b_array, lambda number: None)
 
+        know(0)
         gather_far(0)
+        know(1)
         split_full(0)
         split_turned(0)
         sums[0] = product3(t_high[...], t_low[...], m_high[...], m_low[...])
@@ -395,7 +438,10 @@
         def _():
             sum_near(levels + 1, b_array)
 
+        know(2)
         gather_far(1)
+        for round in range(3, levels - 1):
+            know(round)
         for place in range(4):
             weight_rows(place)
         split_full(1)
@@ -413,16 +459,15 @@
 
             @pl.when(row + step < rows_total)
             def _(stage=stage, step=step, array=array):
+                def arrival(number):
+                    wait_for(piece_of(array, ring, number), entry_sem.at[stage, number])
+
+                sum_own(stage, array, arrival)
+                sum_near(stage, array)
                 if stage > 1:
                     wait_for(full.at[stage], map_sem.at[stage - 1])
                     split_full(stage)
                     split_turned(stage)
-
-                def arrival(number):
-                    wait_for(piece_of(array, ring, number), entry_sem.at[stage, number])
-
-                sum_own(stage, array, arrival)
-                sum_near(stage, array)
                 sum_far(stage, array)
                 sums[stage] = compose(sums[stage - 1])
 
@@ -497,6 +542,7 @@
             pltpu.SemaphoreType.DMA((levels,)),
             pltpu.SemaphoreType.DMA((4,)),
             pltpu.SemaphoreType.DMA((levels + 4, 3)),
+            pltpu.SemaphoreType.REGULAR((levels - 1,)),
         ],
         compiler_params=pltpu.CompilerParams(
             collective_id=0, has_side_effects=True, vmem_limit_bytes=60 * 1024 * 1024

time: 79.8 us -> 78.5 us (0.984)
  Pallas kernels: 78.1 us -> 76.8 us
    pallas_call x1, Pallas kernels: 78.1 us -> 76.8 us  [on_device(): pl.pallas_call(functools.partial(kernel, rows_total, levels), out_shape=j...]
where the time goes in v5:
time: 78.5 us; the launch traced here: 78.4 us
  Pallas kernels  76.8 us (98%)
  local copies, waits for them, and re-layouts  1.57 us (2%)
    pallas_call x1, Pallas kernels, on_device(): pl.pallas_call(functools.partial(kernel, rows_total, levels), out_shape=j...  76.8 us

profile of v5, /device:TPU:1, one launch (start us, length us, event | category | flops | bytes accessed | tf_op | source)
XLA Modules:
  0.0 78.4 jit_solution(7428928016071649522)
XLA Ops:
  0.0 76.8 %shard_map.37 = f32[1,64,512]{2,1,0:T(8,128)} custom-call(f32[1,64,512]{2,1,0:T(8,128)} %d_ref.1, f32[1,64,512]{2,1,0:T(8,128)} %s_ref.1, f32[64,512]{1,0:T(8,128)} %b_ref.1), custom_call_target="tpu_custom_call" | custom-call | tf_op jit(solution)/shard_map/pallas_call | solution.py:524
  76.8 1.6 %copy.5 = f32[1,64,512]{2,1,0:T(8,128)} copy(f32[1,64,512]{2,1,0:T(8,128)} %shard_map.37) | data formatting | bytes 262144

commit v6 on v5

--- a/solution.py
+++ b/solution.py
@@ -483,11 +483,8 @@
             sums.at[levels, pl.ds(0, chunk)], o_ref.at[0],
             send_sem.at[0, 0], misc_sem.at[0], partner,
         )
-        lower = pltpu.make_async_copy(
-            sums.at[levels, pl.ds(chunk, chunk)], o_ref.at[0], misc_sem.at[1]
-        )
         upper.start()
-        lower.start()
+        o_ref[0] = sums[levels, pl.ds(chunk, chunk)]
 
         for stage in range(levels):
             @pl.when(row + 2**stage < rows_total)
@@ -505,7 +502,6 @@
 
         for kind in range(2):
             wait_sent(send_sem.at[levels + 1 + kind, 0], 2, 12 * piece)
-        lower.wait()
         upper.wait_send()
 
     for kind in range(2):
@@ -525,7 +521,7 @@
         functools.partial(kernel, rows_total, levels),
         out_shape=jax.ShapeDtypeStruct(diag_tiles.shape, F32),
         in_specs=[pl.BlockSpec(memory_space=pl.ANY)] * 3,
-        out_specs=pl.BlockSpec(memory_space=pl.ANY),
+        out_specs=pl.BlockSpec(memory_space=pltpu.VMEM),
         scratch_shapes=[
             pltpu.VMEM((arrays, size, size), F32),
             pltpu.VMEM((levels + 1, block, size), F32),
@@ -545,7 +541,7 @@
             pltpu.SemaphoreType.REGULAR((levels - 1,)),
         ],
         compiler_params=pltpu.CompilerParams(
-            collective_id=0, has_side_effects=True, vmem_limit_bytes=60 * 1024 * 1024
+            collective_id=0, has_side_effects=True, vmem_limit_bytes=55040 * 1024
         ),
     )(diag_tiles, sub_tiles, boundary)
 

time: 78.5 us -> 77.4 us (0.986)
  local copies, waits for them, and re-layouts: 1.57 us -> 0.66 us
    unnamed x1, local copies, waits for them, and re-layouts: 1.57 us -> 0.66 us
where the time goes in v6:
time: 77.4 us; the launch traced here: 77.3 us
  Pallas kernels  76.7 us (99%)
    pallas_call x1, Pallas kernels, on_device(): pl.pallas_call(functools.partial(kernel, rows_total, levels), out_shape=j...  76.7 us

profile of v6, /device:TPU:1, one launch (start us, length us, event | category | flops | bytes accessed | tf_op | source)
XLA Modules:
  0.0 77.3 jit_solution(18130564886988503586)
XLA Ops:
  0.0 76.7 %shard_map.37 = f32[1,64,512]{2,1,0:T(8,128)S(1)} custom-call(f32[1,64,512]{2,1,0:T(8,128)} %d_ref.1, f32[1,64,512]{2,1,0:T(8,128)} %s_ref.1, f32[64,512]{1,0:T(8,128)} %b_ref.1), custom_call_target="tpu_custom_call" | custom-call | tf_op jit(solution)/shard_map/pallas_call | solution.py:520
  76.7 0.7 copy.5

commit v7 on v6

--- a/solution.py
+++ b/solution.py
@@ -247,12 +247,12 @@
                     )
                 rows = rows_of(ring, block)
                 full[array, rows] = times_full(full[maps_end + stage, rows])
+                if stage < levels - 1:
+                    pass_map(stage)
                 for eighth in (0, 2, 4, 6, 1, 3, 5, 7):
                     other = eighth + 1 - 2 * (eighth % 2)
                     send(ring, eighth, to_right, eighth)
                     send(ring, other, to_left, 8 + other)
-                if stage < levels - 1:
-                    pass_map(stage)
                 for eighth in range(8):
                     hand_over(ring, eighth)
 

time: 77.4 us -> 77.4 us (level)
  no operation moved by 1% of the time
where the time goes in v7:
time: 77.4 us; the launch traced here: 77.3 us
  Pallas kernels  76.7 us (99%)
    pallas_call x1, Pallas kernels, on_device(): pl.pallas_call(functools.partial(kernel, rows_total, levels), out_shape=j...  76.7 us

profile of v7, /device:TPU:1, one launch (start us, length us, event | category | flops | bytes accessed | tf_op | source)
XLA Modules:
  0.0 77.3 jit_solution(8431044117666368393)
XLA Ops:
  0.0 76.7 %shard_map.37 = f32[1,64,512]{2,1,0:T(8,128)S(1)} custom-call(f32[1,64,512]{2,1,0:T(8,128)} %d_ref.1, f32[1,64,512]{2,1,0:T(8,128)} %s_ref.1, f32[64,512]{1,0:T(8,128)} %b_ref.1), custom_call_target="tpu_custom_call" | custom-call | tf_op jit(solution)/shard_map/pallas_call | solution.py:520
  76.7 0.7 copy.5
